TPU v7x, 32 devices: a whole 2x2x4 slice. The times are simulated.
32 devices in a mesh: gx: 4 (over z), gy: 2 (over y), gz: 4 (over x, core).
Axes of the slice: x: 2, y: 2, z: 4, core: 2. Of those that a mesh axis runs over, the one named last changes fastest.
Arguments:
- positions: float32 [3, 8, 4, 32, 128], P(None, 'gx', 'gy', 'gz'), may hold values from 0 to 1
- shield: float32 [8, 4, 32, 128], P('gx', 'gy', 'gz'), may hold values from 0.3 to 1
- width: float32 [8, 4, 32, 128], P('gx', 'gy', 'gz'), may hold values from 0.5 to 2
- hardness: float32 [8, 4, 32, 128], P('gx', 'gy', 'gz'), may hold values from 0.5 to 2
- softness: float32 [8, 4, 32, 128], P('gx', 'gy', 'gz'), may hold values from 0.5 to 2
- coupling: float32 [8, 4, 32, 128], P('gx', 'gy', 'gz'), may hold values from -0.45 to 0.45
- pair_bits: int32 [8, 4, 32], P('gx', 'gy', 'gz'), may hold values from 8192 to 134217727
- right_side: float32 [4, 8, 4, 32, 128], P(None, 'gx', 'gy', 'gz'), may hold values from -7 to 7
Outputs:
- solution: float32 [4, 8, 4, 32, 128], P(None, 'gx', 'gy', 'gz')
- residual: float32 [4, 8, 4, 32, 128], P(None, 'gx', 'gy', 'gz')
All inputs are finite; a program needn't handle non-finite values.
Results may differ from a plain program's by a relative error of at most 0.0018.
Values sent between devices are 32-bit elements; how exact they have to be, the bound alone decides.
No kernel may reach another device: no remote copies, remote signals or barrier semaphores. Data moves between devices by JAX's collectives and lax.ppermute only.
A program may use at most 128 MiB of HBM per device.

v0:
```python
import jax
import jax.numpy as jnp
from jax import lax
from jax.sharding import PartitionSpec as P

ITERS = 3
coulomb_scale = 0.002
response_scale = 0.003


def extended(block, sides, width):
    for axis, dim in sides:
        count = lax.axis_size(axis)
        forward = [(i, i + 1) for i in range(count - 1)]
        backward = [(target, source) for source, target in forward]
        low = lax.ppermute(
            lax.slice_in_dim(block, block.shape[dim] - width, None, axis=dim), axis, forward
        )
        high = lax.ppermute(lax.slice_in_dim(block, 0, width, axis=dim), axis, backward)
        block = jnp.concatenate([low, block, high], axis=dim)
    return block


def index_tuple(values):
    return tuple((jnp.asarray(value).astype(jnp.int32) for value in values))


def pair_terms(own_params, partner, offset_code, own_bits):
    shift_first = (offset_code // 9 - 1).astype(jnp.float32)
    shift_second = (offset_code // 3 % 3 - 1).astype(jnp.float32)
    shift_third = (offset_code % 3 - 1).astype(jnp.float32)

    def separation(column, shift):
        return shift + (partner[column][:, None, :] - own_params[column][:, :, None])

    first = separation(0, shift_first)
    second = separation(1, shift_second)
    third = separation(2, shift_third)
    distance = first * first + second * second + third * third
    coulomb = coulomb_scale * lax.rsqrt(
        distance + own_params[3][:, :, None] * partner[3][:, None, :]
    )
    response = response_scale * jnp.exp(
        -distance / (own_params[4][:, :, None] + partner[4][:, None, :])
    )
    listed = jnp.right_shift(own_bits, offset_code) & 1 > 0
    tile_size = own_params.shape[2]
    diagonal_mask = lax.broadcasted_iota(
        jnp.int32, (tile_size, tile_size), 0
    ) == lax.broadcasted_iota(jnp.int32, (tile_size, tile_size), 1)
    kept = listed[:, None, None] & jnp.logical_not(diagonal_mask[None] & (offset_code == 13))
    empty_pair = jnp.zeros_like(distance)
    return (
        jnp.where(kept, coulomb, empty_pair).astype(jnp.bfloat16),
        jnp.where(kept, response, empty_pair).astype(jnp.bfloat16),
    )


def tile_block(padded, offset_code, extent):
    fields = padded.shape[0]
    tile_size = padded.shape[4]
    start = index_tuple((0, offset_code // 9, offset_code // 3 % 3, offset_code % 3, 0))
    block = lax.dynamic_slice(padded, start, (fields, extent[0], extent[1], extent[2], tile_size))
    return block.reshape(fields, extent[0] * extent[1] * extent[2], tile_size)


def static_block(padded, offset_code, extent):
    first = offset_code // 9
    second = offset_code // 3 % 3
    third = offset_code % 3
    block = padded[
        :, first : first + extent[0], second : second + extent[1], third : third + extent[2]
    ]
    return block.reshape(padded.shape[0], extent[0] * extent[1] * extent[2], padded.shape[4])


def spread_ghosts(vector, extent):
    shaped = vector.reshape(4, extent[0], extent[1], extent[2], vector.shape[2])
    return extended(shaped, (("gx", 1), ("gy", 2), ("gz", 3)), 1)


def split_parts(padded):
    upper = padded.astype(jnp.bfloat16)
    lower = (padded - upper.astype(jnp.float32)).astype(jnp.bfloat16)
    return jnp.concatenate([upper[:2], lower[:2], upper[2:], lower[2:]], axis=0)


def inner_local(vector, other_vector):
    return jnp.sum((vector * other_vector).reshape(2, 2, -1), axis=(0, 2))


def two_products(vector, applied):
    return lax.psum((inner_local(vector, vector), inner_local(vector, applied)), ("gx", "gy", "gz"))


def widen(scalars):
    return jnp.concatenate([scalars, scalars]).reshape(4, 1, 1)


def on_device(positions, shield, width, hardness, softness, coupling, pair_bits, right_side):
    tiles_x, tiles_y, tiles_z, tile_size = hardness.shape
    extent = (tiles_x, tiles_y, tiles_z)
    tile_count = tiles_x * tiles_y * tiles_z
    params = jnp.concatenate([positions, shield[None], width[None]], axis=0)
    joined = extended(
        jnp.concatenate([params, right_side], axis=0), (("gx", 1), ("gy", 2), ("gz", 3)), 1
    )
    params_pad = joined[:5]
    first_pad = joined[5:]
    own_params = params_pad[:, 1:-1, 1:-1, 1:-1].reshape(5, tile_count, tile_size)
    own_bits = pair_bits.reshape(tile_count)

    def build(offset_code, carry):
        store_coulomb, store_response, row_coulomb, row_response = carry
        offset_code = offset_code.astype(jnp.int32)
        partner = tile_block(params_pad, offset_code, extent)
        coulomb, response = pair_terms(own_params, partner, offset_code, own_bits)
        store_coulomb = lax.dynamic_update_index_in_dim(store_coulomb, coulomb, offset_code, 0)
        store_response = lax.dynamic_update_index_in_dim(store_response, response, offset_code, 0)
        row_coulomb = row_coulomb + jnp.sum(coulomb.astype(jnp.float32), axis=2)
        row_response = row_response + jnp.sum(response.astype(jnp.float32), axis=2)
        return (store_coulomb, store_response, row_coulomb, row_response)

    store_zeros = jnp.zeros((27, tile_count, tile_size, tile_size), jnp.bfloat16)
    flat_zeros = jnp.zeros((tile_count, tile_size), jnp.float32)
    store_coulomb, store_response, row_coulomb, row_response = lax.fori_loop(
        0, 27, build, (store_zeros, store_zeros, flat_zeros, flat_zeros)
    )
    diagonal_charge = hardness.reshape(tile_count, tile_size) + row_coulomb
    diagonal_potential = softness.reshape(tile_count, tile_size) + row_response
    linking = coupling.reshape(tile_count, tile_size)

    def operate(padded, vector):
        parts_pad = split_parts(padded)
        stacked = jnp.stack(
            [static_block(parts_pad, offset_code, extent) for offset_code in range(27)], axis=0
        )
        charge_terms = jnp.einsum(
            "otij,oftj->fti", store_coulomb, stacked[:, :4], preferred_element_type=jnp.float32
        )
        potential_terms = jnp.einsum(
            "otij,oftj->fti", store_response, stacked[:, 4:], preferred_element_type=jnp.float32
        )
        pair_charge = charge_terms[:2] + charge_terms[2:]
        pair_potential = potential_terms[:2] + potential_terms[2:]
        image_charge = diagonal_charge * vector[:2] + pair_charge + linking * vector[2:]
        image_potential = diagonal_potential * vector[2:] - pair_potential + linking * vector[:2]
        return jnp.concatenate([image_charge, image_potential], axis=0)

    rhs_flat = right_side.reshape(4, tile_count, tile_size)
    solution = jnp.zeros_like(rhs_flat)
    applied = operate(first_pad, rhs_flat)
    norm_now, product = two_products(rhs_flat, applied)
    step_size = norm_now / product
    remainder = rhs_flat
    direction = rhs_flat
    along = applied
    for iteration in range(ITERS):
        solution = solution + widen(step_size) * direction
        remainder = remainder - widen(step_size) * along
        if iteration + 1 < ITERS:
            applied = operate(spread_ghosts(remainder, extent), remainder)
            norm_next, product = two_products(remainder, applied)
            beta_ratio = norm_next / norm_now
            step_size = norm_next / (product - beta_ratio * norm_next / step_size)
            direction = remainder + widen(beta_ratio) * direction
            along = applied + widen(beta_ratio) * along
            norm_now = norm_next
    final_image = operate(spread_ghosts(solution, extent), solution)
    residual = rhs_flat - final_image
    shape_out = (4, tiles_x, tiles_y, tiles_z, tile_size)
    return (solution.reshape(shape_out), residual.reshape(shape_out))


def solution(mesh):
    return jax.shard_map(
        on_device,
        mesh=mesh,
        in_specs=(
            P(None, "gx", "gy", "gz", None),
            P("gx", "gy", "gz", None),
            P("gx", "gy", "gz", None),
            P("gx", "gy", "gz", None),
            P("gx", "gy", "gz", None),
            P("gx", "gy", "gz", None),
            P("gx", "gy", "gz"),
            P(None, "gx", "gy", "gz", None),
        ),
        out_specs=(P(None, "gx", "gy", "gz", None), P(None, "gx", "gy", "gz", None)),
        check_vma=False,
    )
```

profile of v0, /device:TPU:14, one launch (start us, length us, event | category | flops | bytes accessed | tf_op | source)
XLA Modules:
  0.0 627.6 jit_solution(3941174055811860574)
XLA Ops:
  30.8 282.4 %while.23 = (s32[]{:T(128)}, bf16[27,32,128,128]{3,2,0,1:T(8,128)(2,1)}, bf16[27,32,128,128]{3,2,0,1:T(8,128)(2,1)}, f32[32,128]{1,0:T(8,128)S(1)}, f32[32,128]{...) while((s32[]{:T(128)}, ...), condition=%wide.region_6.7_spmd.clone, body=%wide.region_3.6_spmd.clone.sunk | while | flops 26271884 | bytes 2933673 | solution.py:126
  31.0 5.2 fusion.83
  41.5 5.2 fusion.83
  51.9 5.2 fusion.83
  62.4 5.2 fusion.83
  83.4 5.3 fusion.83
  104.3 5.2 fusion.83
  135.7 5.2 fusion.83
  187.9 5.2 fusion.83
  219.3 5.2 fusion.83
  240.2 5.3 fusion.83
  250.7 5.3 fusion.83
  271.7 5.2 fusion.83
  315.7 13.1 %convolution_bitcast_fusion.6 = f32[4,32,128]{2,0,1:T(4,128)S(1)} fusion(bf16[27,32,128,128]{3,2,0,1:T(8,128)(2,1)} %get-tuple-element.243, bf16[27,8,32,128]{3,1,0,2:T(8,128)(2,1)S(1)} %constant_dynamic-update-slice_fusion), kind=kOutput, calls=%fused_computation.39 | convolution fusion | flops 113246208 | bytes 29261824 | tf_op jit(solution)/shard_map/otij,oftj->fti/dot_general | solution.py:141
  328.8 13.4 %convolution_bitcast_fusion.7 = f32[4,32,128]{2,0,1:T(4,128)S(1)} fusion(bf16[27,32,128,128]{3,2,0,1:T(8,128)(2,1)} %get-tuple-element.241, bf16[27,8,32,128]{3,1,0,2:T(8,128)(2,1)S(1)} %constant_dynamic-update-slice_fusion), kind=kOutput, calls=%fused_computation.40 | convolution fusion | flops 113246208 | bytes 29261824 | tf_op jit(solution)/shard_map/otij,oftj->fti/dot_general | solution.py:138
  342.7 39.7 %all-reduce.2 = (f32[2]{0:T(128)S(1)}, f32[2]{0:T(128)S(1)}) all-reduce(f32[2]{0:T(128)S(1)} %reduce_sum.132, f32[2]{0:T(128)S(1)} %reduce_sum.135), channel_id=1, replica_groups=mesh['gx'=4,'gy'=2,'gz'=4] {'gx','gy','gz'}, use_global_device_ids=true, to_apply=%region_2.3 | all-reduce | flops 4 | bytes 32 | tf_op jit(solution)/shard_map/psum | solution.py:93
  410.7 13.1 %convolution_bitcast_fusion.4 = f32[4,32,128]{2,0,1:T(4,128)S(1)} fusion(bf16[27,32,128,128]{3,2,0,1:T(8,128)(2,1)} %get-tuple-element.243, bf16[27,8,32,128]{3,1,0,2:T(8,128)(2,1)S(1)} %constant_dynamic-update-slice_fusion.29), kind=kOutput, calls=%fused_computation.37 | convolution fusion | flops 113246208 | bytes 29261824 | tf_op jit(solution)/shard_map/otij,oftj->fti/dot_general | solution.py:141
  423.8 13.4 %convolution_bitcast_fusion.5 = f32[4,32,128]{2,0,1:T(4,128)S(1)} fusion(bf16[27,32,128,128]{3,2,0,1:T(8,128)(2,1)} %get-tuple-element.241, bf16[27,8,32,128]{3,1,0,2:T(8,128)(2,1)S(1)} %constant_dynamic-update-slice_fusion.29), kind=kOutput, calls=%fused_computation.38 | convolution fusion | flops 113246208 | bytes 29261824 | tf_op jit(solution)/shard_map/otij,oftj->fti/dot_general | solution.py:138
  437.5 39.5 %all-reduce.1 = (f32[2]{0:T(128)S(1)}, f32[2]{0:T(128)S(1)}) all-reduce(f32[2]{0:T(128)S(1)} %reduce_sum.138, f32[2]{0:T(128)S(1)} %reduce_sum.141), channel_id=1, replica_groups=mesh['gx'=4,'gy'=2,'gz'=4] {'gx','gy','gz'}, use_global_device_ids=true, to_apply=%region_12.13 | all-reduce | flops 4 | bytes 32 | tf_op jit(solution)/shard_map/psum | solution.py:93
  505.6 13.4 %convolution_bitcast_fusion.3 = f32[4,32,128]{2,0,1:T(4,128)S(1)} fusion(bf16[27,32,128,128]{3,2,0,1:T(8,128)(2,1)} %get-tuple-element.241, bf16[27,8,32,128]{3,1,0,2:T(8,128)(2,1)S(1)} %constant_dynamic-update-slice_fusion.58), kind=kOutput, calls=%fused_computation.36 | convolution fusion | flops 113246208 | bytes 29261824 | tf_op jit(solution)/shard_map/otij,oftj->fti/dot_general | solution.py:138
  519.0 13.1 %convolution_bitcast_fusion.2 = f32[4,32,128]{2,0,1:T(4,128)S(1)} fusion(bf16[27,32,128,128]{3,2,0,1:T(8,128)(2,1)} %get-tuple-element.243, bf16[27,8,32,128]{3,1,0,2:T(8,128)(2,1)S(1)} %constant_dynamic-update-slice_fusion.58), kind=kOutput, calls=%fused_computation.35 | convolution fusion | flops 113246208 | bytes 29261824 | tf_op jit(solution)/shard_map/otij,oftj->fti/dot_general | solution.py:141
  532.4 39.6 %all-reduce = (f32[2]{0:T(128)S(1)}, f32[2]{0:T(128)S(1)}) all-reduce(f32[2]{0:T(128)S(1)} %reduce_sum.144, f32[2]{0:T(128)S(1)} %reduce_sum.147), channel_id=1, replica_groups=mesh['gx'=4,'gy'=2,'gz'=4] {'gx','gy','gz'}, use_global_device_ids=true, to_apply=%region_18.19 | all-reduce | flops 4 | bytes 32 | tf_op jit(solution)/shard_map/psum | solution.py:93
  600.4 13.4 %convolution_bitcast_fusion.1 = f32[4,32,128]{2,0,1:T(4,128)S(1)} fusion(bf16[27,32,128,128]{3,2,0,1:T(8,128)(2,1)} %get-tuple-element.241, bf16[27,8,32,128]{3,1,0,2:T(8,128)(2,1)S(1)} %constant_dynamic-update-slice_fusion.85), kind=kOutput, calls=%fused_computation.34 | convolution fusion | flops 113246208 | bytes 29261824 | tf_op jit(solution)/shard_map/otij,oftj->fti/dot_general | solution.py:138
  613.8 13.1 %convolution_bitcast_fusion = f32[4,32,128]{2,0,1:T(4,128)S(1)} fusion(bf16[27,32,128,128]{3,2,0,1:T(8,128)(2,1)} %get-tuple-element.243, bf16[27,8,32,128]{3,1,0,2:T(8,128)(2,1)S(1)} %constant_dynamic-update-slice_fusion.85), kind=kOutput, calls=%fused_computation.33 | convolution fusion | flops 113246208 | bytes 29261824 | tf_op jit(solution)/shard_map/otij,oftj->fti/dot_general | solution.py:141
  (562 shorter events, 332.9 us)
Async XLA Ops:
  1.6 6.7 %collective-permute-start.1 = (f32[9,1,2,8,128]{4,3,2,1,0:T(8,128)S(1)}, f32[9,1,2,8,128]{4,3,2,1,0:T(8,128)S(1)}, u32[]{:S(2)}, u32[]{:S(2)}) collective-permute-start(f32[9,1,2,8,128]{4,3,2,1,0:T(8,128)S(1)} %get-tuple-element.453), channel_id=1, source_target_pairs={{8,0},{16,8},{24,16},{9,1},{17,9},{25,17},{10,2},{18,10},{26,18},{... | collective-permute-start | bytes 221192 | tf_op jit(solution)/shard_map/ppermute | solution.py:19
  4.0 6.2 collective-permute-start
  11.2 5.1 collective-permute-start.3
  13.6 7.0 %collective-permute-start.2 = (f32[9,4,1,8,128]{4,3,2,1,0:T(8,128)S(1)}, f32[9,4,1,8,128]{4,3,2,1,0:T(8,128)S(1)}, u32[]{:S(2)}, u32[]{:S(2)}) collective-permute-start(f32[9,4,1,8,128]{4,3,2,1,0:T(8,128)S(1)} %get-tuple-element.428), channel_id=1, source_target_pairs={{0,4},{1,5},{2,6},{3,7},{8,12},{9,13},{10,14},{11,15},{16,20},{17,... | collective-permute-start | bytes 442376 | tf_op jit(solution)/shard_map/ppermute | solution.py:16
  20.8 4.4 collective-permute-start.5
  22.7 5.7 collective-permute-start.4
  382.7 5.9 collective-permute-start.7
  385.2 5.8 collective-permute-start.6
  391.0 5.7 collective-permute-start.9
  394.9 6.2 collective-permute-start.8
  401.1 4.7 collective-permute-start.11
  403.0 5.2 collective-permute-start.10
  477.5 5.9 collective-permute-start.13
  480.1 5.8 collective-permute-start.12
  486.0 5.7 collective-permute-start.15
  489.8 6.2 collective-permute-start.14
  496.0 4.4 collective-permute-start.17
  497.9 5.2 collective-permute-start.16
  572.3 5.9 collective-permute-start.19
  574.9 5.8 collective-permute-start.18
  580.8 5.7 collective-permute-start.21
  584.6 6.2 collective-permute-start.20
  590.8 4.5 collective-permute-start.23
  592.7 5.2 collective-permute-start.22
  (11 other events, 156.1 us)
where the time goes:
time: 629 us; the launch traced here: 628 us
  other arithmetic  283 us (45%)
  blocking collectives  119 us (19%)
  matrix products  106 us (17%)
  starting transfers between devices  59.9 us (10%)
  waiting for transfers between devices  40.2 us (6%)
  local copies, waits for them, and re-layouts  12.7 us (2%)
    dynamic_update_slice x27, other arithmetic, build(): lax.dynamic_update_index_in_dim(store_response, response, offset_code, 0)  141 us
    reduce_sum x27, other arithmetic, build(): row_response = row_response + jnp.sum(response.astype(jnp.float32), axis=2)  135 us
    psum x3, blocking collectives, two_products(): lax.psum((inner_local(vector, vector), inner_local(vector, applied)), ('g...  119 us
    dot_general x4, matrix products, operate(): jnp.einsum('otij,oftj->fti', store_coulomb, stacked[:, :4], preferred_ele...  53.5 us
    dot_general x4, matrix products, operate(): jnp.einsum('otij,oftj->fti', store_response, stacked[:, 4:], preferred_el...  52.3 us
    ppermute x12, waiting for transfers between devices, extended(): lax.ppermute(lax.slice_in_dim(block, block.shape[dim] - width, None, axis...  37.8 us
    ppermute x12, starting transfers between devices, extended(): lax.ppermute(lax.slice_in_dim(block, 0, width, axis=dim), axis, backward)  31.7 us
    ppermute x12, starting transfers between devices, extended(): lax.ppermute(lax.slice_in_dim(block, block.shape[dim] - width, None, axis...  28.2 us
  transfers between devices with their start and end apart: 24, of which 16 were waited for; matrix products, arithmetic and copies ran while one was open for 0% of the time, Pallas kernels for 0%

commit v1 on v0

--- a/solution.py
+++ b/solution.py
@@ -90,7 +90,9 @@
 
 
 def two_products(vector, applied):
-    return lax.psum((inner_local(vector, vector), inner_local(vector, applied)), ("gx", "gy", "gz"))
+    return lax.psum(
+        lax.psum((inner_local(vector, vector), inner_local(vector, applied)), ("gy", "gz")), "gx"
+    )
 
 
 def widen(scalars):

time: 629 us -> 568 us (0.903)
  blocking collectives: 119 us -> 55.8 us
  waiting for transfers between devices: 40.2 us -> 47.7 us
    psum x3, blocking collectives: 119 us -> 30.8 us  [two_products(): lax.psum((inner_local(vector, vector), inner_local(vector, applied)), ('g...]
    psum x0 -> x3, blocking collectives: none -> 25 us  [two_products(): lax.psum(lax.psum((inner_local(vector, vector), inner_local(vector, appli...]
    ppermute x12, waiting for transfers between devices: 37.8 us -> 45.3 us  [extended(): lax.ppermute(lax.slice_in_dim(block, block.shape[dim] - width, None, axis...]
where the time goes in v1:
time: 568 us; the launch traced here: 566 us
  other arithmetic  283 us (50%)
  matrix products  105 us (18%)
  blocking collectives  55.8 us (10%)
  starting transfers between devices  54.7 us (10%)
  waiting for transfers between devices  47.7 us (8%)
  local copies, waits for them, and re-layouts  12.7 us (2%)
    dynamic_update_slice x27, other arithmetic, build(): lax.dynamic_update_index_in_dim(store_response, response, offset_code, 0)  141 us
    reduce_sum x27, other arithmetic, build(): row_response = row_response + jnp.sum(response.astype(jnp.float32), axis=2)  135 us
    dot_general x4, matrix products, operate(): jnp.einsum('otij,oftj->fti', store_response, stacked[:, 4:], preferred_el...  52.7 us
    dot_general x4, matrix products, operate(): jnp.einsum('otij,oftj->fti', store_coulomb, stacked[:, :4], preferred_ele...  52.4 us
    ppermute x12, waiting for transfers between devices, extended(): lax.ppermute(lax.slice_in_dim(block, block.shape[dim] - width, None, axis...  45.3 us
    psum x3, blocking collectives, two_products(): lax.psum((inner_local(vector, vector), inner_local(vector, applied)), ('g...  30.8 us
    ppermute x12, starting transfers between devices, extended(): lax.ppermute(lax.slice_in_dim(block, 0, width, axis=dim), axis, backward)  30.5 us
    psum x3, blocking collectives, two_products(): lax.psum(lax.psum((inner_local(vector, vector), inner_local(vector, appli...  25 us
  transfers between devices with their start and end apart: 24, of which 16 were waited for; matrix products, arithmetic and copies ran while one was open for 0% of the time, Pallas kernels for 0%

profile of v1, /device:TPU:14, one launch (start us, length us, event | category | flops | bytes accessed | tf_op | source)
XLA Modules:
  0.0 566.4 jit_solution(12287271475754004539)
XLA Ops:
  30.9 282.5 %while.23 = (s32[]{:T(128)}, bf16[27,32,128,128]{3,2,0,1:T(8,128)(2,1)}, bf16[27,32,128,128]{3,2,0,1:T(8,128)(2,1)}, f32[32,128]{1,0:T(8,128)S(1)}, f32[32,128]{...) while((s32[]{:T(128)}, ...), condition=%wide.region_7.8_spmd.clone, body=%wide.region_4.7_spmd.clone.sunk | while | flops 26271884 | bytes 2933673 | solution.py:128
  41.4 5.2 fusion.83
  51.9 5.3 fusion.83
  83.4 5.2 fusion.83
  93.9 5.2 fusion.83
  114.8 5.3 fusion.83
  135.8 5.2 fusion.83
  271.6 5.3 fusion.83
  282.1 5.3 fusion.83
  315.9 13.2 %convolution_bitcast_fusion.6 = f32[4,32,128]{2,0,1:T(4,128)S(1)} fusion(bf16[27,32,128,128]{3,2,0,1:T(8,128)(2,1)} %get-tuple-element.243, bf16[27,8,32,128]{3,1,0,2:T(8,128)(2,1)S(1)} %constant_dynamic-update-slice_fusion), kind=kOutput, calls=%fused_computation.39 | convolution fusion | flops 113246208 | bytes 29261824 | tf_op jit(solution)/shard_map/otij,oftj->fti/dot_general | solution.py:143
  329.1 13.1 %convolution_bitcast_fusion.7 = f32[4,32,128]{2,0,1:T(4,128)S(1)} fusion(bf16[27,32,128,128]{3,2,0,1:T(8,128)(2,1)} %get-tuple-element.241, bf16[27,8,32,128]{3,1,0,2:T(8,128)(2,1)S(1)} %constant_dynamic-update-slice_fusion), kind=kOutput, calls=%fused_computation.40 | convolution fusion | flops 113246208 | bytes 29261824 | tf_op jit(solution)/shard_map/otij,oftj->fti/dot_general | solution.py:140
  342.7 10.3 %all-reduce.2 = (f32[2]{0:T(128)S(1)}, f32[2]{0:T(128)S(1)}) all-reduce(f32[2]{0:T(128)S(1)} %reduce_sum.132, f32[2]{0:T(128)S(1)} %reduce_sum.135), channel_id=1, replica_groups=mesh['gx'=4,'gy'=2,'gz'=4] {'gy','gz'}, use_global_device_ids=true, to_apply=%region_2.3 | all-reduce | flops 4 | bytes 32 | tf_op jit(solution)/shard_map/psum | solution.py:94
  353.0 9.0 %all-reduce.5 = (f32[2]{0:T(128)S(1)}, f32[2]{0:T(128)S(1)}) all-reduce(f32[2]{0:T(128)S(1)} %get-tuple-element.295, f32[2]{0:T(128)S(1)} %get-tuple-element.296), channel_id=1, replica_groups=mesh['gx'=4,'gy'=2,'gz'=4] {'gx'}, use_global_device_ids=true, to_apply=%region_3.4 | all-reduce | flops 4 | bytes 32 | tf_op jit(solution)/shard_map/psum | solution.py:93
  362.3 5.3 collective-permute-start.7
  392.1 13.2 %convolution_bitcast_fusion.4 = f32[4,32,128]{2,0,1:T(4,128)S(1)} fusion(bf16[27,32,128,128]{3,2,0,1:T(8,128)(2,1)} %get-tuple-element.243, bf16[27,8,32,128]{3,1,0,2:T(8,128)(2,1)S(1)} %constant_dynamic-update-slice_fusion.29), kind=kOutput, calls=%fused_computation.37 | convolution fusion | flops 113246208 | bytes 29261824 | tf_op jit(solution)/shard_map/otij,oftj->fti/dot_general | solution.py:143
  405.3 13.1 %convolution_bitcast_fusion.5 = f32[4,32,128]{2,0,1:T(4,128)S(1)} fusion(bf16[27,32,128,128]{3,2,0,1:T(8,128)(2,1)} %get-tuple-element.241, bf16[27,8,32,128]{3,1,0,2:T(8,128)(2,1)S(1)} %constant_dynamic-update-slice_fusion.29), kind=kOutput, calls=%fused_computation.38 | convolution fusion | flops 113246208 | bytes 29261824 | tf_op jit(solution)/shard_map/otij,oftj->fti/dot_general | solution.py:140
  418.7 10.3 %all-reduce.1 = (f32[2]{0:T(128)S(1)}, f32[2]{0:T(128)S(1)}) all-reduce(f32[2]{0:T(128)S(1)} %reduce_sum.138, f32[2]{0:T(128)S(1)} %reduce_sum.141), channel_id=1, replica_groups=mesh['gx'=4,'gy'=2,'gz'=4] {'gy','gz'}, use_global_device_ids=true, to_apply=%region_14.15 | all-reduce | flops 4 | bytes 32 | tf_op jit(solution)/shard_map/psum | solution.py:94
  429.0 8.0 %all-reduce.4 = (f32[2]{0:T(128)S(1)}, f32[2]{0:T(128)S(1)}) all-reduce(f32[2]{0:T(128)S(1)} %get-tuple-element.293, f32[2]{0:T(128)S(1)} %get-tuple-element.294), channel_id=1, replica_groups=mesh['gx'=4,'gy'=2,'gz'=4] {'gx'}, use_global_device_ids=true, to_apply=%region_15.16 | all-reduce | flops 4 | bytes 32 | tf_op jit(solution)/shard_map/psum | solution.py:93
  465.7 13.1 %convolution_bitcast_fusion.3 = f32[4,32,128]{2,0,1:T(4,128)S(1)} fusion(bf16[27,32,128,128]{3,2,0,1:T(8,128)(2,1)} %get-tuple-element.241, bf16[27,8,32,128]{3,1,0,2:T(8,128)(2,1)S(1)} %constant_dynamic-update-slice_fusion.58), kind=kOutput, calls=%fused_computation.36 | convolution fusion | flops 113246208 | bytes 29261824 | tf_op jit(solution)/shard_map/otij,oftj->fti/dot_general | solution.py:140
  478.8 13.2 %convolution_bitcast_fusion.2 = f32[4,32,128]{2,0,1:T(4,128)S(1)} fusion(bf16[27,32,128,128]{3,2,0,1:T(8,128)(2,1)} %get-tuple-element.243, bf16[27,8,32,128]{3,1,0,2:T(8,128)(2,1)S(1)} %constant_dynamic-update-slice_fusion.58), kind=kOutput, calls=%fused_computation.35 | convolution fusion | flops 113246208 | bytes 29261824 | tf_op jit(solution)/shard_map/otij,oftj->fti/dot_general | solution.py:143
  492.3 10.3 %all-reduce = (f32[2]{0:T(128)S(1)}, f32[2]{0:T(128)S(1)}) all-reduce(f32[2]{0:T(128)S(1)} %reduce_sum.144, f32[2]{0:T(128)S(1)} %reduce_sum.147), channel_id=1, replica_groups=mesh['gx'=4,'gy'=2,'gz'=4] {'gy','gz'}, use_global_device_ids=true, to_apply=%region_22.23 | all-reduce | flops 4 | bytes 32 | tf_op jit(solution)/shard_map/psum | solution.py:94
  502.6 8.0 %all-reduce.3 = (f32[2]{0:T(128)S(1)}, f32[2]{0:T(128)S(1)}) all-reduce(f32[2]{0:T(128)S(1)} %get-tuple-element.291, f32[2]{0:T(128)S(1)} %get-tuple-element.292), channel_id=1, replica_groups=mesh['gx'=4,'gy'=2,'gz'=4] {'gx'}, use_global_device_ids=true, to_apply=%region_23.24 | all-reduce | flops 4 | bytes 32 | tf_op jit(solution)/shard_map/psum | solution.py:93
  539.4 13.1 %convolution_bitcast_fusion.1 = f32[4,32,128]{2,0,1:T(4,128)S(1)} fusion(bf16[27,32,128,128]{3,2,0,1:T(8,128)(2,1)} %get-tuple-element.241, bf16[27,8,32,128]{3,1,0,2:T(8,128)(2,1)S(1)} %constant_dynamic-update-slice_fusion.85), kind=kOutput, calls=%fused_computation.34 | convolution fusion | flops 113246208 | bytes 29261824 | tf_op jit(solution)/shard_map/otij,oftj->fti/dot_general | solution.py:140
  552.5 13.2 %convolution_bitcast_fusion = f32[4,32,128]{2,0,1:T(4,128)S(1)} fusion(bf16[27,32,128,128]{3,2,0,1:T(8,128)(2,1)} %get-tuple-element.243, bf16[27,8,32,128]{3,1,0,2:T(8,128)(2,1)S(1)} %constant_dynamic-update-slice_fusion.85), kind=kOutput, calls=%fused_computation.33 | convolution fusion | flops 113246208 | bytes 29261824 | tf_op jit(solution)/shard_map/otij,oftj->fti/dot_general | solution.py:143
  (565 shorter events, 351.0 us)
Async XLA Ops:
  1.6 6.7 %collective-permute-start.1 = (f32[9,1,2,8,128]{4,3,2,1,0:T(8,128)S(1)}, f32[9,1,2,8,128]{4,3,2,1,0:T(8,128)S(1)}, u32[]{:S(2)}, u32[]{:S(2)}) collective-permute-start(f32[9,1,2,8,128]{4,3,2,1,0:T(8,128)S(1)} %get-tuple-element.459), channel_id=1, source_target_pairs={{8,0},{16,8},{24,16},{9,1},{17,9},{25,17},{10,2},{18,10},{26,18},{... | collective-permute-start | bytes 221192 | tf_op jit(solution)/shard_map/ppermute | solution.py:19
  4.0 6.2 %collective-permute-start = (f32[9,1,2,8,128]{4,3,2,1,0:T(8,128)S(1)}, f32[9,1,2,8,128]{4,3,2,1,0:T(8,128)S(1)}, u32[]{:S(2)}, u32[]{:S(2)}) collective-permute-start(f32[9,1,2,8,128]{4,3,2,1,0:T(8,128)S(1)} %get-tuple-element.458), channel_id=1, source_target_pairs={{0,8},{8,16},{16,24},{1,9},{9,17},{17,25},{2,10},{10,18},{18,26},{... | collective-permute-start | bytes 221192 | tf_op jit(solution)/shard_map/ppermute | solution.py:16
  11.2 5.1 collective-permute-start.3
  13.6 7.0 %collective-permute-start.2 = (f32[9,4,1,8,128]{4,3,2,1,0:T(8,128)S(1)}, f32[9,4,1,8,128]{4,3,2,1,0:T(8,128)S(1)}, u32[]{:S(2)}, u32[]{:S(2)}) collective-permute-start(f32[9,4,1,8,128]{4,3,2,1,0:T(8,128)S(1)} %get-tuple-element.434), channel_id=1, source_target_pairs={{0,4},{1,5},{2,6},{3,7},{8,12},{9,13},{10,14},{11,15},{16,20},{17,... | collective-permute-start | bytes 442376 | tf_op jit(solution)/shard_map/ppermute | solution.py:16
  20.8 4.4 collective-permute-start.5
  22.7 5.7 %collective-permute-start.4 = (f32[9,4,4,1,128]{4,3,2,1,0:T(1,128)S(1)}, f32[9,4,4,1,128]{4,3,2,1,0:T(1,128)S(1)}, u32[]{:S(2)}, u32[]{:S(2)}) collective-permute-start(f32[9,4,4,1,128]{4,3,2,1,0:T(1,128)S(1)} %get-tuple-element.324), channel_id=1, source_target_pairs={{0,1},{1,2},{2,3},{4,5},{5,6},{6,7},{8,9},{9,10},{10,11},{12,13},{... | collective-permute-start | bytes 221192 | tf_op jit(solution)/shard_map/ppermute | solution.py:16
  362.3 7.3 %collective-permute-start.7 = (f32[4,1,2,8,128]{4,3,2,1,0:T(8,128)S(1)}, f32[4,1,2,8,128]{4,3,2,1,0:T(8,128)S(1)}, u32[]{:S(2)}, u32[]{:S(2)}) collective-permute-start(f32[4,1,2,8,128]{4,3,2,1,0:T(8,128)S(1)} %get-tuple-element.483), channel_id=1, source_target_pairs={{8,0},{16,8},{24,16},{9,1},{17,9},{25,17},{10,2},{18,10},{26,18},{... | collective-permute-start | bytes 98312 | tf_op jit(solution)/shard_map/ppermute | solution.py:19
  367.6 5.8 %collective-permute-start.6 = (f32[4,1,2,8,128]{4,3,2,1,0:T(8,128)S(1)}, f32[4,1,2,8,128]{4,3,2,1,0:T(8,128)S(1)}, u32[]{:S(2)}, u32[]{:S(2)}) collective-permute-start(f32[4,1,2,8,128]{4,3,2,1,0:T(8,128)S(1)} %get-tuple-element.482), channel_id=1, source_target_pairs={{0,8},{8,16},{16,24},{1,9},{9,17},{17,25},{2,10},{10,18},{18,26},{... | collective-permute-start | bytes 98312 | tf_op jit(solution)/shard_map/ppermute | solution.py:16
  373.4 3.2 collective-permute-start.9
  374.8 6.2 %collective-permute-start.8 = (f32[4,4,1,8,128]{4,3,2,1,0:T(8,128)S(1)}, f32[4,4,1,8,128]{4,3,2,1,0:T(8,128)S(1)}, u32[]{:S(2)}, u32[]{:S(2)}) collective-permute-start(f32[4,4,1,8,128]{4,3,2,1,0:T(8,128)S(1)} %get-tuple-element.464), channel_id=1, source_target_pairs={{0,4},{1,5},{2,6},{3,7},{8,12},{9,13},{10,14},{11,15},{16,20},{17,... | collective-permute-start | bytes 196616 | tf_op jit(solution)/shard_map/ppermute | solution.py:16
  381.0 4.7 collective-permute-start.11
  382.9 6.8 %collective-permute-start.10 = (f32[4,4,4,1,128]{4,3,2,1,0:T(1,128)S(1)}, f32[4,4,4,1,128]{4,3,2,1,0:T(1,128)S(1)}, u32[]{:S(2)}, u32[]{:S(2)}) collective-permute-start(f32[4,4,4,1,128]{4,3,2,1,0:T(1,128)S(1)} %get-tuple-element.452), channel_id=1, source_target_pairs={{0,1},{1,2},{2,3},{4,5},{5,6},{6,7},{8,9},{9,10},{10,11},{12,13},{... | collective-permute-start | bytes 98312 | tf_op jit(solution)/shard_map/ppermute | solution.py:16
  437.5 6.2 %collective-permute-start.13 = (f32[4,1,2,8,128]{4,3,2,1,0:T(8,128)S(1)}, f32[4,1,2,8,128]{4,3,2,1,0:T(8,128)S(1)}, u32[]{:S(2)}, u32[]{:S(2)}) collective-permute-start(f32[4,1,2,8,128]{4,3,2,1,0:T(8,128)S(1)} %get-tuple-element.481), channel_id=1, source_target_pairs={{8,0},{16,8},{24,16},{9,1},{17,9},{25,17},{10,2},{18,10},{26,18},{... | collective-permute-start | bytes 98312 | tf_op jit(solution)/shard_map/ppermute | solution.py:19
  441.8 5.8 %collective-permute-start.12 = (f32[4,1,2,8,128]{4,3,2,1,0:T(8,128)S(1)}, f32[4,1,2,8,128]{4,3,2,1,0:T(8,128)S(1)}, u32[]{:S(2)}, u32[]{:S(2)}) collective-permute-start(f32[4,1,2,8,128]{4,3,2,1,0:T(8,128)S(1)} %get-tuple-element.480), channel_id=1, source_target_pairs={{0,8},{8,16},{16,24},{1,9},{9,17},{17,25},{2,10},{10,18},{18,26},{... | collective-permute-start | bytes 98312 | tf_op jit(solution)/shard_map/ppermute | solution.py:16
  447.6 3.2 collective-permute-start.15
  448.9 6.2 %collective-permute-start.14 = (f32[4,4,1,8,128]{4,3,2,1,0:T(8,128)S(1)}, f32[4,4,1,8,128]{4,3,2,1,0:T(8,128)S(1)}, u32[]{:S(2)}, u32[]{:S(2)}) collective-permute-start(f32[4,4,1,8,128]{4,3,2,1,0:T(8,128)S(1)} %get-tuple-element.462), channel_id=1, source_target_pairs={{0,4},{1,5},{2,6},{3,7},{8,12},{9,13},{10,14},{11,15},{16,20},{17,... | collective-permute-start | bytes 196616 | tf_op jit(solution)/shard_map/ppermute | solution.py:16
  455.1 4.4 collective-permute-start.17
  457.1 6.2 %collective-permute-start.16 = (f32[4,4,4,1,128]{4,3,2,1,0:T(1,128)S(1)}, f32[4,4,4,1,128]{4,3,2,1,0:T(1,128)S(1)}, u32[]{:S(2)}, u32[]{:S(2)}) collective-permute-start(f32[4,4,4,1,128]{4,3,2,1,0:T(1,128)S(1)} %get-tuple-element.446), channel_id=1, source_target_pairs={{0,1},{1,2},{2,3},{4,5},{5,6},{6,7},{8,9},{9,10},{10,11},{12,13},{... | collective-permute-start | bytes 98312 | tf_op jit(solution)/shard_map/ppermute | solution.py:16
  510.9 6.2 %collective-permute-start.19 = (f32[4,1,2,8,128]{4,3,2,1,0:T(8,128)S(1)}, f32[4,1,2,8,128]{4,3,2,1,0:T(8,128)S(1)}, u32[]{:S(2)}, u32[]{:S(2)}) collective-permute-start(f32[4,1,2,8,128]{4,3,2,1,0:T(8,128)S(1)} %get-tuple-element.477), channel_id=1, source_target_pairs={{8,0},{16,8},{24,16},{9,1},{17,9},{25,17},{10,2},{18,10},{26,18},{... | collective-permute-start | bytes 98312 | tf_op jit(solution)/shard_map/ppermute | solution.py:19
  515.2 5.8 %collective-permute-start.18 = (f32[4,1,2,8,128]{4,3,2,1,0:T(8,128)S(1)}, f32[4,1,2,8,128]{4,3,2,1,0:T(8,128)S(1)}, u32[]{:S(2)}, u32[]{:S(2)}) collective-permute-start(f32[4,1,2,8,128]{4,3,2,1,0:T(8,128)S(1)} %get-tuple-element.476), channel_id=1, source_target_pairs={{0,8},{8,16},{16,24},{1,9},{9,17},{17,25},{2,10},{10,18},{18,26},{... | collective-permute-start | bytes 98312 | tf_op jit(solution)/shard_map/ppermute | solution.py:16
  521.0 3.2 collective-permute-start.21
  522.4 6.2 %collective-permute-start.20 = (f32[4,4,1,8,128]{4,3,2,1,0:T(8,128)S(1)}, f32[4,4,1,8,128]{4,3,2,1,0:T(8,128)S(1)}, u32[]{:S(2)}, u32[]{:S(2)}) collective-permute-start(f32[4,4,1,8,128]{4,3,2,1,0:T(8,128)S(1)} %get-tuple-element.460), channel_id=1, source_target_pairs={{0,4},{1,5},{2,6},{3,7},{8,12},{9,13},{10,14},{11,15},{16,20},{17,... | collective-permute-start | bytes 196616 | tf_op jit(solution)/shard_map/ppermute | solution.py:16
  528.6 4.7 collective-permute-start.23
  530.7 6.2 %collective-permute-start.22 = (f32[4,4,4,1,128]{4,3,2,1,0:T(1,128)S(1)}, f32[4,4,4,1,128]{4,3,2,1,0:T(1,128)S(1)}, u32[]{:S(2)}, u32[]{:S(2)}) collective-permute-start(f32[4,4,4,1,128]{4,3,2,1,0:T(1,128)S(1)} %get-tuple-element.440), channel_id=1, source_target_pairs={{0,1},{1,2},{2,3},{4,5},{5,6},{6,7},{8,9},{9,10},{10,11},{12,13},{... | collective-permute-start | bytes 98312 | tf_op jit(solution)/shard_map/ppermute | solution.py:16
  (11 other events, 155.5 us)
